TPU v7x, 128 devices: a whole 4x4x4 slice. The times are simulated.
128 devices in a mesh: fsdp: 32 (over z, y, x_hi), sp: 4 (over x_lo, core).
Axes of the slice: x: 4 (x_hi: 2, x_lo: 2; x = x_hi * 2 + x_lo), y: 4, z: 4, core: 2. Of those that a mesh axis runs over, the one named last changes fastest.
Arguments:
- tokens: bfloat16 [32, 512, 1536], P('fsdp', 'sp'), may hold values from -6 to 6
- modulation: float32 [32, 1, 6, 1536], P('fsdp'), may hold values from -4 to 4
- w_qkv: bfloat16 [1, 1536, 3, 1536], P(None, 'fsdp', None, 'sp'), may hold values from -0.15625 to 0.15625
- w_out: bfloat16 [1, 1536, 1536], P(None, 'sp', 'fsdp'), may hold values from -0.15625 to 0.15625
- w_in: bfloat16 [1, 1536, 6144], P(None, 'fsdp', 'sp'), may hold values from -0.15625 to 0.15625
- w_back: bfloat16 [1, 6144, 1536], P(None, 'sp', 'fsdp'), may hold values from -0.078125 to 0.078125
- out_grad: bfloat16 [32, 512, 1536], P('fsdp', 'sp'), may hold values from -6 to 6
Outputs:
- final_out: bfloat16 [32, 512, 1536], P('fsdp', 'sp')
- input_grad: float32 [32, 512, 1536], P('fsdp', 'sp')
- grad_qkv: float32 [1, 1536, 3, 1536], P(None, 'fsdp', None, 'sp')
- grad_out: float32 [1, 1536, 1536], P(None, 'sp', 'fsdp')
- grad_in: float32 [1, 1536, 6144], P(None, 'fsdp', 'sp')
- grad_back: float32 [1, 6144, 1536], P(None, 'sp', 'fsdp')
All inputs are finite; a program needn't handle non-finite values.
Results may differ from a plain program's by a relative error of at most 0.03.
Values may be sent and summed in bfloat16 or wider, within the bound.
A program may use at most 128 MiB of HBM per device.

v0:
```python
import math
import jax
import jax.numpy as jnp
from jax import lax
from jax.sharding import PartitionSpec as P

HEAD_DIM = 128
LN_EPS = 1e-06
TEMPER = 2.5


def normalize(x):
    c = x - jnp.mean(x, axis=-1, keepdims=True)
    r = lax.rsqrt(jnp.mean(c * c, axis=-1, keepdims=True) + LN_EPS)
    return (c * r, r)


def norm_back(n, r, e):
    return r * (
        e - jnp.mean(e, axis=-1, keepdims=True) - n * jnp.mean(e * n, axis=-1, keepdims=True)
    )


def dot(a, b, ca, cb):
    return lax.dot_general(a, b, (((ca,), (cb,)), ((), ())), preferred_element_type=jnp.float32)


def bf(x):
    return x.astype(jnp.bfloat16)


def body(tokens, modulation, w_qkv, w_out, w_in, w_back, out_grad):
    seq, width = tokens.shape[1:]
    own = w_qkv.shape[3]
    heads = own // HEAD_DIM
    ff = w_in.shape[2]
    c = TEMPER / math.sqrt(HEAD_DIM)
    q_s = 1.0 / math.sqrt(seq * lax.axis_size("fsdp") * lax.axis_size("sp"))
    mod = modulation[0, 0]
    m = [mod[i : i + 1] for i in range(6)]
    rows = w_qkv.shape[1]
    weights = [
        lax.all_gather(w, "fsdp", axis=0, tiled=True)
        for w in (w_qkv[0].reshape(rows, 3 * own), w_out[0].T, w_in[0], w_back[0].T)
    ]
    wq, wo, wi, wb = weights

    def gather(v):
        return lax.all_gather(v, "sp", axis=0, tiled=True)

    def scatter(v):
        return lax.psum_scatter(bf(v), "sp", scatter_dimension=0, tiled=True).astype(jnp.float32)

    x = tokens[0].astype(jnp.float32)
    dx = out_grad[0].astype(jnp.float32)
    n1, r1 = normalize(x)
    a1 = gather(bf(n1 * (1.0 + m[1]) + m[0]))
    dm = gather(bf(m[5] * dx))
    qkv = bf(dot(a1, wq, 1, 0))

    def attend(h):
        q, k, v = (qkv[:, i * own + h * HEAD_DIM : i * own + (h + 1) * HEAD_DIM] for i in range(3))
        p = jax.nn.softmax(dot(q, k, 1, 1) * c, axis=-1)
        return (q, k, v, p)

    o = jnp.concatenate(
        [bf(dot(bf(p), v, 1, 0)) for q, k, v, p in map(attend, range(heads))], axis=1
    )
    mid = x + m[2] * scatter(dot(o, wo, 1, 1))
    n2, r2 = normalize(mid)
    a2 = gather(bf(n2 * (1.0 + m[4]) + m[3]))
    u = dot(a2, wi, 1, 0)
    act, pull = jax.vjp(lambda t: jax.nn.gelu(t, approximate=True), u)
    g = bf(act)
    final = bf(mid + m[5] * scatter(dot(g, wb, 1, 1)))
    du = bf(pull(dot(dm, wb, 1, 0))[0])
    dmid = dx + norm_back(n2, r2, scatter(dot(du, wi, 1, 1)) * (1.0 + m[4]))
    da = gather(bf(m[2] * dmid))
    do = bf(dot(da, wo, 1, 0))
    dq, dk, dv = ([], [], [])
    for h in range(heads):
        q, k, v, p = attend(h)
        doh = do[:, h * HEAD_DIM : (h + 1) * HEAD_DIM]
        dp = dot(doh, v, 1, 1)
        ds = bf(c * p * (dp - jnp.sum(p * dp, axis=-1, keepdims=True)))
        dq.append(bf(dot(ds, k, 1, 0)))
        dk.append(bf(dot(ds, q, 0, 0)))
        dv.append(bf(dot(bf(p), doh, 0, 0)))
    dqkv = jnp.concatenate(dq + dk + dv, axis=1)
    dxin = dmid + norm_back(n1, r1, scatter(dot(dqkv, wq, 1, 1)) * (1.0 + m[1]))

    def reduce(a, b):
        g = bf(dot(a, b, 0, 0) * q_s)
        return lax.psum_scatter(g, "fsdp", scatter_dimension=0, tiled=True).astype(jnp.float32)

    gb = reduce(dm, g)
    gi = reduce(a2, du)
    go = reduce(da, o)
    gq = reduce(a1, dqkv)
    return (final[None], dxin[None], gq.reshape(1, rows, 3, own), go.T[None], gi[None], gb.T[None])


def solution(mesh):
    return jax.shard_map(
        body,
        mesh=mesh,
        in_specs=(
            P("fsdp", "sp", None),
            P("fsdp", None, None, None),
            P(None, "fsdp", None, "sp"),
            P(None, "sp", "fsdp"),
            P(None, "fsdp", "sp"),
            P(None, "sp", "fsdp"),
            P("fsdp", "sp", None),
        ),
        out_specs=(
            P("fsdp", "sp", None),
            P("fsdp", "sp", None),
            P(None, "fsdp", None, "sp"),
            P(None, "sp", "fsdp"),
            P(None, "fsdp", "sp"),
            P(None, "sp", "fsdp"),
        ),
        check_vma=False,
    )
```

profile of v0, /device:TPU:0, one launch (start us, length us, event | category | flops | bytes accessed | tf_op | source)
XLA Modules:
  0.0 1512.2 jit_solution(13099963642387650823)
XLA Ops:
  7.2 1.1 convert_reduce_fusion
  8.4 1.3 fusion.47
  10.5 2.1 fusion.41
  14.2 25.6 %all-gather.10.cloned.1.call-done = bf16[512,1536]{1,0:T(8,128)(2,1)} async-done(((bf16[128,1536]{1,0:T(8,128)(2,1)}), bf16[512,1536]{1,0:T(8,128)(2,1)}) %all-gather.10.cloned.1.call-update) | async-done | bytes 1572880 | tf_op jit(solution)/shard_map/all_gather | solution.py:49
  39.8 81.9 %all-gather.12.cloned.1.call-done = bf16[1536,1152]{1,0:T(8,128)(2,1)} async-done(((bf16[48,1152]{1,0:T(8,128)(2,1)}), bf16[1536,1152]{1,0:T(8,128)(2,1)}) %all-gather.12.cloned.1.call-update) | async-done | bytes 3538960 | tf_op jit(solution)/shard_map/all_gather | solution.py:43
  121.7 4.7 convolution_convert_fusion.1
  129.1 61.7 %all-gather.14.cloned.1.call-done = bf16[1536,384]{1,0:T(8,128)(2,1)} async-done(((bf16[48,384]{1,0:T(8,128)(2,1)}), bf16[1536,384]{1,0:T(8,128)(2,1)}) %all-gather.14.cloned.1.call-update) | async-done | bytes 1179664 | tf_op jit(solution)/shard_map/all_gather | solution.py:43
  190.8 3.4 convolution_convert_fusion.3
  197.4 18.1 %reduce-scatter.9.cloned.1.call-done = bf16[128,1536]{1,0:T(8,128)(2,1)} async-done(((bf16[512,1536]{1,0:T(8,128)(2,1)}), bf16[128,1536]{1,0:T(8,128)(2,1)}) %reduce-scatter.9.cloned.1.call-update) | async-done | bytes 393232 | tf_op jit(solution)/shard_map/reduce_scatter | solution.py:52
  215.5 1.3 fusion.52
  216.8 1.3 multiply_reduce_fusion.4
  219.2 24.0 %all-gather.20.cloned.1.call-done = bf16[512,1536]{1,0:T(8,128)(2,1)} async-done(((bf16[128,1536]{1,0:T(8,128)(2,1)}), bf16[512,1536]{1,0:T(8,128)(2,1)}) %all-gather.20.cloned.1.call-update) | async-done | bytes 1572880 | tf_op jit(solution)/shard_map/all_gather | solution.py:49
  243.1 86.9 %all-gather.18.cloned.1.call-done = bf16[1536,1536]{1,0:T(8,128)(2,1)} async-done(((bf16[48,1536]{1,0:T(8,128)(2,1)}), bf16[1536,1536]{1,0:T(8,128)(2,1)}) %all-gather.18.cloned.1.call-update) | async-done | bytes 4718608 | tf_op jit(solution)/shard_map/all_gather | solution.py:43
  330.0 7.1 fusion.97
  337.2 77.5 %all-gather.24.cloned.1.call-done = bf16[1,1536,1536]{2,1,0:T(8,128)(2,1)} async-done(((bf16[1,48,1536]{2,1,0:T(8,128)(2,1)}), bf16[1,1536,1536]{2,1,0:T(8,128)(2,1)}) %all-gather.24.cloned.1.call-update) | async-done | bytes 4718608 | tf_op jit(solution)/shard_map/all_gather | solution.py:43
  414.7 25.5 %all-gather.16.cloned.1.call-done = bf16[512,1536]{1,0:T(8,128)(2,1)} async-done(((bf16[128,1536]{1,0:T(8,128)(2,1)}), bf16[512,1536]{1,0:T(8,128)(2,1)}) %all-gather.16.cloned.1.call-update) | async-done | bytes 1572880 | tf_op jit(solution)/shard_map/all_gather | solution.py:49
  440.2 9.7 fusion.13
  449.9 1.2 copy-done.44
  451.1 3.8 fusion.14
  455.2 7.3 convolution_convert_fusion.2
  462.6 17.5 %reduce-scatter.13.cloned.1.call-done = bf16[128,1536]{1,0:T(8,128)(2,1)} async-done(((bf16[512,1536]{1,0:T(8,128)(2,1)}), bf16[128,1536]{1,0:T(8,128)(2,1)}) %reduce-scatter.13.cloned.1.call-update) | async-done | bytes 393232 | tf_op jit(solution)/shard_map/reduce_scatter | solution.py:52
  480.1 1.4 fusion.50
  481.5 25.7 %reduce-scatter.11.cloned.1.call-done = bf16[128,1536]{1,0:T(8,128)(2,1)} async-done(((bf16[512,1536]{1,0:T(8,128)(2,1)}), bf16[128,1536]{1,0:T(8,128)(2,1)}) %reduce-scatter.11.cloned.1.call-update) | async-done | bytes 393232 | tf_op jit(solution)/shard_map/reduce_scatter | solution.py:52
  507.2 2.9 multiply_convert_fusion.4
  510.1 25.6 %all-gather.22.cloned.1.call-done = bf16[512,1536]{1,0:T(8,128)(2,1)} async-done(((bf16[128,1536]{1,0:T(8,128)(2,1)}), bf16[512,1536]{1,0:T(8,128)(2,1)}) %all-gather.22.cloned.1.call-update) | async-done | bytes 1572880 | tf_op jit(solution)/shard_map/all_gather | solution.py:49
  535.7 2.7 convolution_convert_fusion.4
  538.5 2.9 multiply_reduce_fusion
  541.4 2.9 multiply_reduce_fusion.1
  544.3 2.9 multiply_reduce_fusion.2
  547.2 2.0 fusion.17
  549.4 1.7 multiply_convert_fusion.3
  557.3 3.4 convolution_convert_fusion
  560.8 1.3 copy-done.32
  562.1 4.4 fusion
  566.8 1.1 copy-done.31
  567.9 6.8 fusion.1
  574.8 1.3 copy-done.30
  576.4 4.1 fusion.2
  580.5 196.6 %reduce-scatter.19.cloned.1.call-done = bf16[48,384]{1,0:T(8,128)(2,1)} async-done(((bf16[1536,384]{1,0:T(8,128)(2,1)}), bf16[48,384]{1,0:T(8,128)(2,1)}) %reduce-scatter.19.cloned.1.call-update) | async-done | bytes 36880 | tf_op jit(solution)/shard_map/reduce_scatter | solution.py:94
  777.1 1.4 convert_bitcast_fusion.2
  778.6 21.9 %reduce-scatter.15.cloned.1.call-done = bf16[128,1536]{1,0:T(8,128)(2,1)} async-done(((bf16[512,1536]{1,0:T(8,128)(2,1)}), bf16[128,1536]{1,0:T(8,128)(2,1)}) %reduce-scatter.15.cloned.1.call-update) | async-done | bytes 393232 | tf_op jit(solution)/shard_map/reduce_scatter | solution.py:52
  800.5 1.3 fusion.49
  801.8 2.2 fusion.46
  804.0 234.6 %reduce-scatter.21.cloned.1.call-done = bf16[48,1536]{1,0:T(8,128)(2,1)} async-done(((bf16[1536,1536]{1,0:T(8,128)(2,1)}), bf16[48,1536]{1,0:T(8,128)(2,1)}) %reduce-scatter.21.cloned.1.call-update) | async-done | bytes 147472 | tf_op jit(solution)/shard_map/reduce_scatter | solution.py:94
  1038.6 1.6 bitcast_convert_fusion
  1040.2 232.4 %reduce-scatter.23.cloned.1.call-done = bf16[48,1536]{1,0:T(8,128)(2,1)} async-done(((bf16[1536,1536]{1,0:T(8,128)(2,1)}), bf16[48,1536]{1,0:T(8,128)(2,1)}) %reduce-scatter.23.cloned.1.call-update) | async-done | bytes 147472 | tf_op jit(solution)/shard_map/reduce_scatter | solution.py:94
  1272.6 1.6 convert_bitcast_fusion.1
  1274.2 229.8 %reduce-scatter.17.cloned.1.call-done = bf16[48,1152]{1,0:T(8,128)(2,1)} async-done(((bf16[1536,1152]{1,0:T(8,128)(2,1)}), bf16[48,1152]{1,0:T(8,128)(2,1)}) %reduce-scatter.17.cloned.1.call-update) | async-done | bytes 110608 | tf_op jit(solution)/shard_map/reduce_scatter | solution.py:94
  (154 shorter events, 18.4 us)
Async XLA Ops:
  7.2 5.5 copy-start.10
  7.2 32.6 %all-gather.10.cloned.1.call-start = ((), (), s32[]{:S(2)}) async-start(), calls=%async_computation.8 | async-start | bytes 1966080 | tf_op jit(solution)/shard_map/all_gather | solution.py:49
  8.4 118.0 %copy-start.22 = (f32[128]{0:T(128)}, f32[128]{0:T(128)S(1)}, u32[]{:S(2)}) copy-start(f32[128]{0:T(128)S(1)} %broadcast_multiply_fusion.5) | copy-start | bytes 1540
  9.6 116.7 %copy-start.24 = (f32[128]{0:T(128)}, f32[128]{0:T(128)S(1)}, u32[]{:S(2)}) copy-start(f32[128]{0:T(128)S(1)} %add_rsqrt_fusion.1) | copy-start | bytes 1540
  12.6 109.1 %all-gather.12.cloned.1.call-start = ((), (), s32[]{:S(2)}) async-start(), calls=%async_computation.9 | async-start | bytes 3649536 | tf_op jit(solution)/shard_map/all_gather | solution.py:43
  13.4 177.3 %all-gather.14.cloned.1.call-start = ((), (), s32[]{:S(2)}) async-start(), calls=%async_computation.10 | async-start | bytes 1216512 | tf_op jit(solution)/shard_map/all_gather | solution.py:43
  14.1 201.4 %reduce-scatter.9.cloned.1.call-start = ((), (), s32[]{:S(2)}) async-start(), calls=%async_computation.11 | async-start | bytes 1966080 | tf_op jit(solution)/shard_map/reduce_scatter | solution.py:52
  126.4 2.3 copy-start.6
  126.9 411.6 %copy-start.14 = (f32[512]{0:T(512)}, f32[512]{0:T(512)S(1)}, u32[]{:S(2)}) copy-start(f32[512]{0:T(512)S(1)} %fusion.39) | copy-start | bytes 6148
  128.3 62.4 %copy-start.36 = (bf16[512,128]{0,1:T(8,128)(2,1)}, bf16[512,128]{0,1:T(8,128)(2,1)S(1)}, u32[]{:S(2)}) copy-start(bf16[512,128]{0,1:T(8,128)(2,1)S(1)} %convolution_convert_fusion.14) | copy-start | bytes 393220
  128.7 62.0 %copy-start.38 = (bf16[512,128]{0,1:T(8,128)(2,1)}, bf16[512,128]{0,1:T(8,128)(2,1)S(1)}, u32[]{:S(2)}) copy-start(bf16[512,128]{0,1:T(8,128)(2,1)S(1)} %convolution_convert_fusion.15) | copy-start | bytes 393220
  129.1 61.7 %copy-start.40 = (bf16[512,128]{0,1:T(8,128)(2,1)}, bf16[512,128]{0,1:T(8,128)(2,1)S(1)}, u32[]{:S(2)}) copy-start(bf16[512,128]{0,1:T(8,128)(2,1)S(1)} %convolution_convert_fusion.16) | copy-start | bytes 393220
  194.2 21.3 %copy-start = (bf16[1,128,1536]{2,1,0:T(8,128)(2,1)S(1)}, bf16[1,128,1536]{2,1,0:T(8,128)(2,1)}, u32[]{:S(2)}) copy-start(bf16[1,128,1536]{2,1,0:T(8,128)(2,1)} %param.7) | copy-start | bytes 1179652
  194.2 48.9 %all-gather.20.cloned.1.call-start = ((), (), s32[]{:S(2)}) async-start(), calls=%async_computation.15 | async-start | bytes 1966080 | tf_op jit(solution)/shard_map/all_gather | solution.py:49
  196.0 134.0 %all-gather.18.cloned.1.call-start = ((), (), s32[]{:S(2)}) async-start(), calls=%async_computation.13 | async-start | bytes 4866048 | tf_op jit(solution)/shard_map/all_gather | solution.py:43
  196.6 218.1 %all-gather.24.cloned.1.call-start = ((), (), s32[]{:S(2)}) async-start(), calls=%async_computation.23 | async-start | bytes 4866048 | tf_op jit(solution)/shard_map/all_gather | solution.py:43
  197.4 242.8 %all-gather.16.cloned.1.call-start = ((), (), s32[]{:S(2)}) async-start(), calls=%async_computation.12 | async-start | bytes 1966080 | tf_op jit(solution)/shard_map/all_gather | solution.py:49
  215.5 2.6 copy-start.1
  219.1 261.0 %reduce-scatter.13.cloned.1.call-start = ((), (), s32[]{:S(2)}) async-start(), calls=%async_computation.16 | async-start | bytes 1966080 | tf_op jit(solution)/shard_map/reduce_scatter | solution.py:52
  440.2 10.9 copy-start.28
  455.0 52.2 %reduce-scatter.11.cloned.1.call-start = ((), (), s32[]{:S(2)}) async-start(), calls=%async_computation.14 | async-start | bytes 1966080 | tf_op jit(solution)/shard_map/reduce_scatter | solution.py:52
  462.5 73.2 %all-gather.22.cloned.1.call-start = ((), (), s32[]{:S(2)}) async-start(), calls=%async_computation.17 | async-start | bytes 1966080 | tf_op jit(solution)/shard_map/all_gather | solution.py:49
  510.1 267.1 %reduce-scatter.19.cloned.1.call-start = ((), (), s32[]{:S(2)}) async-start(), calls=%async_computation.20 | async-start | bytes 1216512 | tf_op jit(solution)/shard_map/reduce_scatter | solution.py:94
  538.5 5.8 copy-start.42
  538.5 2.9 copy-start.17
  541.4 2.9 copy-start.3
  541.4 2.9 copy-start.12
  541.4 2.9 copy-start.20
  544.3 2.9 copy-start.33
  544.3 2.9 copy-start.37
  544.3 2.9 copy-start.39
  544.3 2.9 copy-start.41
  549.3 251.2 %reduce-scatter.15.cloned.1.call-start = ((), (), s32[]{:S(2)}) async-start(), calls=%async_computation.18 | async-start | bytes 1966080 | tf_op jit(solution)/shard_map/reduce_scatter | solution.py:52
  549.3 1.7 copy-start.7
  549.4 2.0 copy-start.9
  549.4 2.0 copy-start.15
  549.4 2.0 copy-start.27
  554.9 2.4 copy-start.29
  557.3 3.5 copy-start.45
  560.7 477.8 %reduce-scatter.21.cloned.1.call-start = ((), (), s32[]{:S(2)}) async-start(), calls=%async_computation.21 | async-start | bytes 4866048 | tf_op jit(solution)/shard_map/reduce_scatter | solution.py:94
  566.5 1.4 copy-start.31
  566.5 706.1 %reduce-scatter.23.cloned.1.call-start = ((), (), s32[]{:S(2)}) async-start(), calls=%async_computation.22 | async-start | bytes 4866048 | tf_op jit(solution)/shard_map/reduce_scatter | solution.py:94
  574.7 1.4 copy-start.30
  574.7 1.8 copy-start.35
  574.7 929.3 %reduce-scatter.17.cloned.1.call-start = ((), (), s32[]{:S(2)}) async-start(), calls=%async_computation.19 | async-start | bytes 3649536 | tf_op jit(solution)/shard_map/reduce_scatter | solution.py:94
  580.5 220.0 %copy-start.23 = (f32[128]{0:T(128)S(1)}, f32[128]{0:T(128)}, u32[]{:S(2)}) copy-start(f32[128]{0:T(128)} %copy-done.22) | copy-start | bytes 1540
  580.5 220.0 %copy-start.25 = (f32[128]{0:T(128)S(1)}, f32[128]{0:T(128)}, u32[]{:S(2)}) copy-start(f32[128]{0:T(128)} %copy-done.24) | copy-start | bytes 1540
  580.5 221.3 %copy-start.4 = (f32[128,1536]{1,0:T(8,128)S(1)}, f32[128,1536]{1,0:T(8,128)}, u32[]{:S(2)}) copy-start(f32[128,1536]{1,0:T(8,128)} %get-tuple-element.29) | copy-start | bytes 2359300
  (14 other events, 15.8 us)
Sparse Core Ops, SparseCore 0:
  12.7 27.0 all-gather.9
  43.4 78.2 all-gather.11
  124.7 65.9 all-gather.13
  194.3 21.1 reduce-scatter.8
  217.6 25.4 all-gather.19
  246.0 83.9 all-gather.17
  333.1 81.5 all-gather.23
  416.9 23.2 all-gather.15
  455.1 24.9 reduce-scatter.12
  482.3 24.7 reduce-scatter.10
  510.2 25.4 all-gather.21
  549.4 227.6 reduce-scatter.18
  779.6 20.8 reduce-scatter.14
  805.4 233.1 reduce-scatter.20
  1043.5 229.0 reduce-scatter.22
  1277.4 226.5 reduce-scatter.16
where the time goes:
time: 1510 us
  waiting for transfers between devices  1390 us (92%)
  matrix products  72.8 us (5%)
  other arithmetic  25 us (2%)
    reduce_scatter x4, waiting for transfers between devices, reduce(): lax.psum_scatter(g, 'fsdp', scatter_dimension=0, tiled=True)  893 us
    all_gather x4, waiting for transfers between devices, body(): lax.all_gather(w, 'fsdp', axis=0, tiled=True)  308 us
    all_gather x4, waiting for transfers between devices, gather(): return lax.all_gather(v, 'sp', axis=0, tiled=True)  101 us
    reduce_scatter x4, waiting for transfers between devices, scatter(): lax.psum_scatter(bf(v), 'sp', scatter_dimension=0, tiled=True)  83.3 us
    dot_general x30, matrix products, dot(): lax.dot_general(a, b, (((ca,), (cb,)), ((), ())), preferred_element_type=...  72.8 us
  transfers between devices with their start and end apart: 16, of which 16 were waited for; matrix products, arithmetic and copies ran while one was open for 4% of the time, Pallas kernels for 0%

commit v1 on v0

--- a/solution.py
+++ b/solution.py
@@ -40,7 +40,9 @@
     m = [mod[i : i + 1] for i in range(6)]
     rows = w_qkv.shape[1]
     weights = [
-        lax.all_gather(w, "fsdp", axis=0, tiled=True)
+        jnp.concatenate(
+            lax.all_to_all(jnp.stack([w] * lax.axis_size("fsdp")), "fsdp", 0, 0), axis=0
+        )
         for w in (w_qkv[0].reshape(rows, 3 * own), w_out[0].T, w_in[0], w_back[0].T)
     ]
     wq, wo, wi, wb = weights

time: 1510 us -> 1330 us (0.88)
  waiting for transfers between devices: 1390 us -> 1160 us
  starting transfers between devices: 1.06 us -> 26.4 us
    all_gather x4 -> x0, waiting for transfers between devices: 308 us -> none  [body(): lax.all_gather(w, 'fsdp', axis=0, tiled=True)]
    all_to_all x0 -> x4, waiting for transfers between devices: none -> 183 us  [body(): lax.all_to_all(jnp.stack([w] * lax.axis_size('fsdp')), 'fsdp', 0, 0)]
    all_gather x4, waiting for transfers between devices: 101 us -> 25.6 us  [gather(): return lax.all_gather(v, 'sp', axis=0, tiled=True)]
    all_to_all x0 -> x4, starting transfers between devices: none -> 25.5 us  [body(): lax.all_to_all(jnp.stack([w] * lax.axis_size('fsdp')), 'fsdp', 0, 0)]
    reduce_scatter x4, waiting for transfers between devices: 83.3 us -> 60.4 us  [scatter(): lax.psum_scatter(bf(v), 'sp', scatter_dimension=0, tiled=True)]
  transfers between devices with their start and end apart: 16 -> 16, of which waited for: 16 -> 12; matrix products, arithmetic and copies ran while one was open for 4% -> 6% of each run, Pallas kernels for 0% -> 0%
where the time goes in v1:
time: 1330 us
  waiting for transfers between devices  1160 us (87%)
  matrix products  83.4 us (6%)
  starting transfers between devices  26.4 us (2%)
  other arithmetic  23.5 us (2%)
  local copies, waits for them, and re-layouts  21.4 us (2%)
  between operations  14.9 us (1%)
    reduce_scatter x4, waiting for transfers between devices, reduce(): lax.psum_scatter(g, 'fsdp', scatter_dimension=0, tiled=True)  890 us
    all_to_all x4, waiting for transfers between devices, body(): lax.all_to_all(jnp.stack([w] * lax.axis_size('fsdp')), 'fsdp', 0, 0)  183 us
    dot_general x30, matrix products, dot(): lax.dot_general(a, b, (((ca,), (cb,)), ((), ())), preferred_element_type=...  83.4 us
    reduce_scatter x4, waiting for transfers between devices, scatter(): lax.psum_scatter(bf(v), 'sp', scatter_dimension=0, tiled=True)  60.4 us
  transfers between devices with their start and end apart: 16, of which 12 were waited for; matrix products, arithmetic and copies ran while one was open for 6% of the time, Pallas kernels for 0%

profile of v1, /device:TPU:0, one launch (start us, length us, event | category | flops | bytes accessed | tf_op | source)
XLA Modules:
  0.0 1328.9 jit_solution(6505821571951696841)
XLA Ops:
  8.1 2.0 stack.8
  10.2 11.1 all-to-all-start
  23.6 56.4 %all-to-all-done = bf16[32,48,1152]{2,1,0:T(8,128)(2,1)} async-done(((bf16[32,48,1152]{2,1,0:T(8,128)(2,1)}), bf16[32,48,1152]{2,1,0:T(8,128)(2,1)}, u32[]{:S(2)}, u32[]{:S(2)}) %all-to-all-start) | async-done | bytes 3538976 | tf_op jit(solution)/shard_map/all_to_all | solution.py:44
  81.1 4.7 all-to-all-start.1
  85.8 4.7 convolution_convert_fusion.1
  93.9 11.5 all-to-all-done.1
  105.4 3.6 stack.11
  109.0 4.9 all-to-all-start.3
  116.9 1.3 convolution_convert_fusion.16
  118.3 1.3 convolution_convert_fusion.17
  120.2 3.5 convolution_convert_fusion.4
  125.6 57.3 %all-to-all-done.3 = bf16[32,48,1536]{2,1,0:T(8,128)(2,1)} async-done(((bf16[32,48,1536]{2,1,0:T(8,128)(2,1)}), bf16[32,48,1536]{2,1,0:T(8,128)(2,1)}, u32[]{:S(2)}, u32[]{:S(2)}) %all-to-all-start.3) | async-done | bytes 4718624 | tf_op jit(solution)/shard_map/all_to_all | solution.py:44
  182.9 2.8 stack.10
  185.7 4.9 all-to-all-start.2
  190.7 1.3 fusion.45
  194.5 7.0 fusion.90
  201.5 58.2 %all-to-all-done.2 = bf16[32,48,1536]{2,1,0:T(8,128)(2,1)} async-done(((bf16[32,48,1536]{2,1,0:T(8,128)(2,1)}), bf16[32,48,1536]{2,1,0:T(8,128)(2,1)}, u32[]{:S(2)}, u32[]{:S(2)}) %all-to-all-start.2) | async-done | bytes 4718624 | tf_op jit(solution)/shard_map/all_to_all | solution.py:44
  259.7 9.5 fusion.9
  270.4 6.1 convolution_convert_fusion.2
  276.6 7.3 convolution_convert_fusion.3
  283.9 12.7 reduce-scatter.13.cloned.1.call-done
  296.6 1.4 fusion.43
  298.0 25.7 %reduce-scatter.11.cloned.1.call-done = bf16[128,1536]{1,0:T(8,128)(2,1)} async-done(((bf16[512,1536]{1,0:T(8,128)(2,1)}), bf16[128,1536]{1,0:T(8,128)(2,1)}) %reduce-scatter.11.cloned.1.call-update) | async-done | bytes 393232 | tf_op jit(solution)/shard_map/reduce_scatter | solution.py:54
  323.7 2.9 multiply_convert_fusion.4
  326.7 25.6 %all-gather.11.cloned.1.call-done = bf16[512,1536]{1,0:T(8,128)(2,1)} async-done(((bf16[128,1536]{1,0:T(8,128)(2,1)}), bf16[512,1536]{1,0:T(8,128)(2,1)}) %all-gather.11.cloned.1.call-update) | async-done | bytes 1572880 | tf_op jit(solution)/shard_map/all_gather | solution.py:51
  352.3 2.7 convolution_convert_fusion.5
  355.0 2.8 multiply_reduce_fusion
  357.9 2.8 multiply_reduce_fusion.1
  360.8 2.9 multiply_reduce_fusion.2
  363.7 2.0 fusion.10
  366.1 1.7 multiply_convert_fusion.3
  373.0 5.4 convolution_convert_fusion
  378.5 1.3 copy-done.41
  379.8 5.7 fusion
  385.6 1.3 copy-done.40
  386.9 6.9 fusion.1
  393.8 1.3 copy-done.39
  395.2 5.3 fusion.2
  400.6 193.1 %reduce-scatter.19.cloned.1.call-done = bf16[48,384]{1,0:T(8,128)(2,1)} async-done(((bf16[1536,384]{1,0:T(8,128)(2,1)}), bf16[48,384]{1,0:T(8,128)(2,1)}) %reduce-scatter.19.cloned.1.call-update) | async-done | bytes 36880 | tf_op jit(solution)/shard_map/reduce_scatter | solution.py:96
  593.6 1.4 convert_bitcast_fusion.2
  595.0 21.9 %reduce-scatter.15.cloned.1.call-done = bf16[128,1536]{1,0:T(8,128)(2,1)} async-done(((bf16[512,1536]{1,0:T(8,128)(2,1)}), bf16[128,1536]{1,0:T(8,128)(2,1)}) %reduce-scatter.15.cloned.1.call-update) | async-done | bytes 393232 | tf_op jit(solution)/shard_map/reduce_scatter | solution.py:54
  617.0 1.3 fusion.42
  618.3 2.2 fusion.39
  620.5 234.5 %reduce-scatter.21.cloned.1.call-done = bf16[48,1536]{1,0:T(8,128)(2,1)} async-done(((bf16[1536,1536]{1,0:T(8,128)(2,1)}), bf16[48,1536]{1,0:T(8,128)(2,1)}) %reduce-scatter.21.cloned.1.call-update) | async-done | bytes 147472 | tf_op jit(solution)/shard_map/reduce_scatter | solution.py:96
  855.0 1.6 bitcast_convert_fusion
  856.6 232.5 %reduce-scatter.23.cloned.1.call-done = bf16[48,1536]{1,0:T(8,128)(2,1)} async-done(((bf16[1536,1536]{1,0:T(8,128)(2,1)}), bf16[48,1536]{1,0:T(8,128)(2,1)}) %reduce-scatter.23.cloned.1.call-update) | async-done | bytes 147472 | tf_op jit(solution)/shard_map/reduce_scatter | solution.py:96
  1089.1 1.6 convert_bitcast_fusion.1
  1090.8 229.6 %reduce-scatter.17.cloned.1.call-done = bf16[48,1152]{1,0:T(8,128)(2,1)} async-done(((bf16[1536,1152]{1,0:T(8,128)(2,1)}), bf16[48,1152]{1,0:T(8,128)(2,1)}) %reduce-scatter.17.cloned.1.call-update) | async-done | bytes 110608 | tf_op jit(solution)/shard_map/reduce_scatter | solution.py:96
  (168 shorter events, 24.4 us)
Async XLA Ops:
  10.1 11.2 copy-start
  10.2 11.4 copy-start.14
  10.2 69.8 %all-to-all-start = ((bf16[32,48,1152]{2,1,0:T(8,128)(2,1)}), bf16[32,48,1152]{2,1,0:T(8,128)(2,1)}, u32[]{:S(2)}, u32[]{:S(2)}) async-start(bf16[32,48,1152]{2,1,0:T(8,128)(2,1)} %stack.8), calls=%async_computation | async-start | bytes 7077888 | tf_op jit(solution)/shard_map/all_to_all | solution.py:44
  21.3 58.7 %copy-start.13 = (bf16[1,384,48]{1,2,0:T(8,128)(2,1)S(1)}, bf16[1,384,48]{1,2,0:T(8,128)(2,1)}, u32[]{:S(2)}) copy-start(bf16[1,384,48]{1,2,0:T(8,128)(2,1)} %param.10) | copy-start | bytes 110596
  21.3 64.5 %all-gather.5.cloned.1.call-start = ((), (), s32[]{:S(2)}) async-start(), calls=%async_computation.12 | async-start | bytes 1966080 | tf_op jit(solution)/shard_map/all_gather | solution.py:51
  22.2 58.9 %copy-start.33 = (f32[128]{0:T(128)}, f32[128]{0:T(128)S(1)}, u32[]{:S(2)}) copy-start(f32[128]{0:T(128)S(1)} %broadcast_multiply_fusion.5) | copy-start | bytes 1540
  22.5 58.6 %copy-start.35 = (f32[128]{0:T(128)}, f32[128]{0:T(128)S(1)}, u32[]{:S(2)}) copy-start(f32[128]{0:T(128)S(1)} %add_rsqrt_fusion.1) | copy-start | bytes 1540
  81.1 24.3 %all-to-all-start.1 = ((bf16[32,48,384]{2,1,0:T(8,128)(2,1)}), bf16[32,48,384]{2,1,0:T(8,128)(2,1)}, u32[]{:S(2)}, u32[]{:S(2)}) async-start(bf16[32,48,384]{2,1,0:T(8,128)(2,1)} %stack.9), calls=%async_computation.1 | async-start | bytes 2359296 | tf_op jit(solution)/shard_map/all_to_all | solution.py:44
  90.5 2.6 copy-start.6
  93.9 24.3 %copy-start.2 = (f32[512,512]{0,1:T(8,128)}, f32[512,512]{0,1:T(8,128)S(1)}, u32[]{:S(2)}) copy-start(f32[512,512]{0,1:T(8,128)S(1)} %get-tuple-element.36) | copy-start | bytes 3145732
  109.0 73.9 %all-to-all-start.3 = ((bf16[32,48,1536]{2,1,0:T(8,128)(2,1)}), bf16[32,48,1536]{2,1,0:T(8,128)(2,1)}, u32[]{:S(2)}, u32[]{:S(2)}) async-start(bf16[32,48,1536]{2,1,0:T(8,128)(2,1)} %stack.11), calls=%async_computation.4 | async-start | bytes 9437184 | tf_op jit(solution)/shard_map/all_to_all | solution.py:44
  113.9 76.7 %reduce-scatter.9.cloned.1.call-start = ((), (), s32[]{:S(2)}) async-start(), calls=%async_computation.13 | async-start | bytes 1966080 | tf_op jit(solution)/shard_map/reduce_scatter | solution.py:54
  114.8 2.1 copy-start.27
  115.6 2.6 copy-start.30
  116.9 2.7 copy-start.44
  123.7 59.2 %copy-start.10 = (bf16[1,48,1536]{2,1,0:T(8,128)(2,1)S(1)}, bf16[1,48,1536]{2,1,0:T(8,128)(2,1)}, u32[]{:S(2)}) copy-start(bf16[1,48,1536]{2,1,0:T(8,128)(2,1)} %param.11) | copy-start | bytes 442372
  123.8 70.7 %all-gather.9.cloned.1.call-start = ((), (), s32[]{:S(2)}) async-start(), calls=%async_computation.16 | async-start | bytes 1966080 | tf_op jit(solution)/shard_map/all_gather | solution.py:51
  185.7 74.0 %all-to-all-start.2 = ((bf16[32,48,1536]{2,1,0:T(8,128)(2,1)}), bf16[32,48,1536]{2,1,0:T(8,128)(2,1)}, u32[]{:S(2)}, u32[]{:S(2)}) async-start(bf16[32,48,1536]{2,1,0:T(8,128)(2,1)} %stack.10), calls=%async_computation.3 | async-start | bytes 9437184 | tf_op jit(solution)/shard_map/all_to_all | solution.py:44
  190.5 2.7 copy-start.11
  190.6 2.7 copy-start.15
  190.6 69.1 %all-gather.7.cloned.1.call-start = ((), (), s32[]{:S(2)}) async-start(), calls=%async_computation.14 | async-start | bytes 1966080 | tf_op jit(solution)/shard_map/all_gather | solution.py:51
  190.6 2.6 copy-start.1
  194.2 102.4 %reduce-scatter.13.cloned.1.call-start = ((), (), s32[]{:S(2)}) async-start(), calls=%async_computation.17 | async-start | bytes 1966080 | tf_op jit(solution)/shard_map/reduce_scatter | solution.py:54
  276.5 47.2 %reduce-scatter.11.cloned.1.call-start = ((), (), s32[]{:S(2)}) async-start(), calls=%async_computation.15 | async-start | bytes 1966080 | tf_op jit(solution)/shard_map/reduce_scatter | solution.py:54
  283.9 68.4 %all-gather.11.cloned.1.call-start = ((), (), s32[]{:S(2)}) async-start(), calls=%async_computation.18 | async-start | bytes 1966080 | tf_op jit(solution)/shard_map/all_gather | solution.py:51
  326.6 28.4 %copy-start.18 = (f32[512]{0:T(512)S(1)}, f32[512]{0:T(512)}, u32[]{:S(2)}) copy-start(f32[512]{0:T(512)} %copy-done.16) | copy-start | bytes 6148
  326.6 28.4 %copy-start.25 = (f32[512]{0:T(512)S(1)}, f32[512]{0:T(512)}, u32[]{:S(2)}) copy-start(f32[512]{0:T(512)} %fusion.32) | copy-start | bytes 6148
  326.6 267.0 %reduce-scatter.19.cloned.1.call-start = ((), (), s32[]{:S(2)}) async-start(), calls=%async_computation.21 | async-start | bytes 1216512 | tf_op jit(solution)/shard_map/reduce_scatter | solution.py:96
  355.0 5.7 copy-start.50
  355.0 2.9 copy-start.20
  355.0 2.9 copy-start.28
  357.9 2.9 copy-start.3
  357.9 2.9 copy-start.22
  357.9 2.9 copy-start.31
  360.7 3.0 copy-start.42
  360.8 2.9 copy-start.45
  360.8 2.9 copy-start.47
  360.8 2.9 copy-start.49
  365.8 251.2 %reduce-scatter.15.cloned.1.call-start = ((), (), s32[]{:S(2)}) async-start(), calls=%async_computation.19 | async-start | bytes 1966080 | tf_op jit(solution)/shard_map/reduce_scatter | solution.py:54
  366.1 2.0 copy-start.9
  366.1 2.0 copy-start.26
  366.1 2.0 copy-start.38
  378.4 476.6 %reduce-scatter.21.cloned.1.call-start = ((), (), s32[]{:S(2)}) async-start(), calls=%async_computation.22 | async-start | bytes 4866048 | tf_op jit(solution)/shard_map/reduce_scatter | solution.py:96
  385.5 703.6 %reduce-scatter.23.cloned.1.call-start = ((), (), s32[]{:S(2)}) async-start(), calls=%async_computation.23 | async-start | bytes 4866048 | tf_op jit(solution)/shard_map/reduce_scatter | solution.py:96
  393.8 926.6 %reduce-scatter.17.cloned.1.call-start = ((), (), s32[]{:S(2)}) async-start(), calls=%async_computation.20 | async-start | bytes 3649536 | tf_op jit(solution)/shard_map/reduce_scatter | solution.py:96
  400.5 216.5 %copy-start.34 = (f32[128]{0:T(128)S(1)}, f32[128]{0:T(128)}, u32[]{:S(2)}) copy-start(f32[128]{0:T(128)} %copy-done.33) | copy-start | bytes 1540
  400.5 216.5 %copy-start.36 = (f32[128]{0:T(128)S(1)}, f32[128]{0:T(128)}, u32[]{:S(2)}) copy-start(f32[128]{0:T(128)} %copy-done.35) | copy-start | bytes 1540
  400.5 217.8 %copy-start.4 = (f32[128,1536]{1,0:T(8,128)S(1)}, f32[128,1536]{1,0:T(8,128)}, u32[]{:S(2)}) copy-start(f32[128,1536]{1,0:T(8,128)} %get-tuple-element.29) | copy-start | bytes 2359300
  (21 other events, 26.2 us)
Sparse Core Ops, SparseCore 0:
  24.4 38.8 all-gather.4
  123.9 38.0 reduce-scatter.8
  164.2 26.0 all-gather.8
  194.4 39.0 all-gather.6
  276.6 19.9 reduce-scatter.12
  298.9 24.7 reduce-scatter.10
  326.7 25.4 all-gather.10
  365.9 227.6 reduce-scatter.18
  596.0 20.8 reduce-scatter.14
  621.9 233.0 reduce-scatter.20
  860.1 229.0 reduce-scatter.22
  1094.0 226.3 reduce-scatter.16
